TPU v7x, 32 devices: a whole 2x2x4 slice. The times are simulated.
32 devices in a mesh: groups: 2 (over y), block: 4 (over z), seg: 2 (over x), sub: 2 (over core).
Axes of the slice: x: 2, y: 2, z: 4, core: 2. Of those that a mesh axis runs over, the one named last changes fastest.
Arguments:
- old_fields: float32 [2048, 4, 512], P(('groups', 'block', 'seg', 'sub')), parts along dimension 0, may hold values from -6 to 6
- corner_shift: float32 [24, 2048], P(None, ('groups', 'block', 'seg', 'sub')), parts along dimension 1, may hold values from -0.2 to 0.2
- targets: float32 [3, 131072], P(None, ('groups', 'block', 'seg', 'sub')), parts along dimension 1, may hold values from -0.7 to 0.7
- owners: int32 [1024], P(('groups', 'block', 'seg', 'sub')), parts along dimension 0, may hold values from 0 to 1023, as said below
Outputs:
- new_fields: float32 [4, 131072], P(None, ('groups', 'block', 'seg', 'sub')), parts along dimension 1
There are 2 independent parts, one for each index of `groups`. A program takes and returns all parts, laid end to end along the dimension named above; each array names one. Nothing has to cross between parts.
Inputs may be any that keep to these rules, and one draw needn't show every extreme that they name: `owners`: owner e lies on device e // 64. At most 2 of the blocks on the rows of one device are owned by elements of any one device, and in every draw some device owns exactly 2 blocks of every device.
All inputs are finite; a program needn't handle non-finite values.
Results may differ from a plain program's by a relative error of at most 0.00029.
Values sent between devices are 32-bit elements; how exact they have to be, the bound alone decides.
A program may use at most 64 MiB of HBM per device.

v0:
```python
import functools

import jax
import jax.numpy as jnp
from jax import lax
from jax.experimental import pallas as pl
from jax.experimental.pallas import tpu as pltpu
from jax.sharding import PartitionSpec as P

NEWTON = 3
CAP = 2
GROUP_PEERS = 4
AXES = ("block", "seg", "sub")

GLL_POINTS = (
    -1.0,
    -0.8717401485096066,
    -0.5917001814331423,
    -0.2092992179024789,
    0.2092992179024789,
    0.5917001814331423,
    0.8717401485096066,
    1.0,
)
WEIGHTS = []
for _n in range(8):
    _w = 1.0
    for _m in range(8):
        if _m != _n:
            _w /= GLL_POINTS[_n] - GLL_POINTS[_m]
    WEIGHTS.append(_w)

F32 = jnp.float32
BF16 = jnp.bfloat16
EXACT = lax.Precision.HIGHEST
NT = (((1,), (1,)), ((), ()))


def iota(shape, dim):
    return lax.broadcasted_iota(jnp.int32, shape, dim)


def flip(index, static):
    bit = 1
    while bit <= static:
        if static & bit:
            index = index + bit * (1 - 2 * ((index // bit) % 2))
        bit *= 2
    return index


def newton(coef, y):
    def update(xi, jac, misfit):
        m = jac
        cof = [
            [m[1][1] * m[2][2] - m[1][2] * m[2][1], m[1][2] * m[2][0] - m[1][0] * m[2][2], m[1][0] * m[2][1] - m[1][1] * m[2][0]],
            [m[0][2] * m[2][1] - m[0][1] * m[2][2], m[0][0] * m[2][2] - m[0][2] * m[2][0], m[0][1] * m[2][0] - m[0][0] * m[2][1]],
            [m[0][1] * m[1][2] - m[0][2] * m[1][1], m[0][2] * m[1][0] - m[0][0] * m[1][2], m[0][0] * m[1][1] - m[0][1] * m[1][0]],
        ]
        inv = 1.0 / (m[0][0] * cof[0][0] + m[0][1] * cof[0][1] + m[0][2] * cof[0][2])
        out = []
        for b in range(3):
            step = (cof[0][b] * misfit[0] + cof[1][b] * misfit[1] + cof[2][b] * misfit[2]) * inv
            new = -step if xi is None else xi[b] - step
            out.append(jnp.clip(new, -1.2, 1.2))
        return out

    xi = update(None, [[c[4], c[2], c[1]] for c in coef], [c[0] - t for c, t in zip(coef, y)])
    for _ in range(NEWTON - 1):
        u, v, w = xi
        uv, uw, vw = u * v, u * w, v * w
        jac, misfit = [], []
        for c, t in zip(coef, y):
            du = c[4] + c[6] * v + c[5] * w + c[7] * vw
            dv = c[2] + c[6] * u + c[3] * w + c[7] * uw
            dw = c[1] + c[5] * u + c[3] * v + c[7] * uv
            jac.append([du, dv, dw])
            misfit.append((c[0] - t) + u * du + v * (c[2] + c[3] * w) + w * c[1])
        xi = update(xi, jac, misfit)
    return xi


def lagrange(x):
    diff = [x - t for t in GLL_POINTS]
    pre = [None, diff[0]]
    for n in range(2, 8):
        pre.append(pre[-1] * diff[n - 1])
    suf = [None] * 8
    suf[6] = diff[7]
    for n in range(5, -1, -1):
        suf[n] = suf[n + 1] * diff[n + 1]
    out = []
    for n in range(8):
        value = suf[n] if n == 0 else pre[n] if n == 7 else pre[n] * suf[n]
        out.append(value * WEIGHTS[n])
    return out


def kernel(sizes, group_peers, owners_hbm, targets_hbm, shift_hbm, fields_hbm, out_ref,
           owners_ref, targets_ref, shift_ref, fbuf, table, send, recv, res, ret, lag, idsend, idrecv, ids, slotv, slots,
           osem, tsem, csem, fsem, idsem, slotsem, s0, r0, s1, r1, s2, r2):
    nb, ns, nc = sizes
    n = nb * ns * nc
    blocks = owners_ref.shape[1]
    elems = shift_ref.shape[1]
    pts = out_ref.shape[2]
    groups = n // group_peers
    lanes = idsend.shape[1]
    wide = idsend.shape[0]
    here = [lax.axis_index(a) for a in AXES]
    me = (here[0] * ns + here[1]) * nc + here[2]

    def peer(k):
        if isinstance(k, int):
            return {
                "block": flip(here[0], k // (ns * nc)),
                "seg": flip(here[1], (k // nc) % ns),
                "sub": flip(here[2], k % nc),
            }
        other = jnp.bitwise_xor(me, k)
        return {"block": other // (ns * nc), "seg": (other // nc) % ns, "sub": other % nc}

    def message(k):
        return pl.ds(8 * k if isinstance(k, int) else pl.multiple_of(8 * k, 8), 3 * CAP)

    def for_wait(first, count, ref, sem):
        part = ref.at[pl.ds(8 * first, 3 * CAP * count), :]
        pltpu.make_async_copy(part, part, sem).wait()

    def send_result(k, g):
        part = pl.ds(CAP * k, CAP)
        return pltpu.make_async_remote_copy(
            src_ref=res.at[part], dst_ref=ret.at[part], send_sem=s2, recv_sem=r2.at[g],
            device_id=peer(k), device_id_type=pl.DeviceIdType.MESH)

    get_owners = pltpu.make_async_copy(owners_hbm, owners_ref, osem)
    get_owners.start()
    get_targets = pltpu.make_async_copy(targets_hbm, targets_ref, tsem)
    get_targets.start()
    get_shift = pltpu.make_async_copy(shift_hbm, shift_ref, csem)
    get_shift.start()
    fetch = pltpu.make_async_copy(fields_hbm, fbuf, fsem)
    fetch.start()
    barrier = pltpu.get_barrier_semaphore()
    unrolled = n <= 32

    def for_peers(first, last, body):
        if unrolled:
            for k in reversed(range(first, last)):
                body(k)
        else:
            lax.fori_loop(first, last, lambda k, c: (body(k), c)[1], 0)

    for_peers(1, n, lambda k: pl.semaphore_signal(
        barrier, inc=1, device_id=peer(k), device_id_type=pl.DeviceIdType.MESH))

    shift_bits = elems.bit_length() - 1
    get_owners.wait()
    own = owners_ref[...]
    owner_dev = jnp.right_shift(own, shift_bits)
    hit = (jnp.bitwise_xor(iota((n, blocks), 0), me) == owner_dev).astype(F32)
    earlier = (iota((blocks, blocks), 0) < iota((blocks, blocks), 1)).astype(F32)
    rank = jnp.dot(hit, earlier, preferred_element_type=F32)
    match = [jnp.where(rank == float(c), hit, 0.0) for c in range(CAP)]
    both = jnp.concatenate(match, axis=0)
    get_targets.wait()
    cat = jnp.concatenate([targets_ref[:, a, :] for a in range(3)], axis=1)
    packed = jnp.dot(both, cat, precision=EXACT, preferred_element_type=F32)
    for c in range(CAP):
        part = slice(c * n, (c + 1) * n)
        for a in range(3):
            send[pl.ds(3 * c + a, n, stride=8), :] = packed[part, a * pts:(a + 1) * pts]
            recv[3 * c + a:3 * c + a + 1, :] = packed[c * n:c * n + 1, a * pts:(a + 1) * pts]
    square = (blocks, blocks)
    diag = iota(square, 0) == iota(square, 1)
    own_rows = jnp.broadcast_to(own, square)
    own_col = jnp.sum(jnp.where(diag, own_rows, 0), axis=1, keepdims=True)
    dev_col = jnp.right_shift(own_col, shift_bits)
    dev_row = jnp.right_shift(own_rows, shift_bits)
    same = jnp.where(dev_col == dev_row, 1, 0)
    rank_row = jnp.sum(jnp.where(iota(square, 0) < iota(square, 1), same, 0), axis=0, keepdims=True)
    rank_col = jnp.sum(jnp.where(iota(square, 1) < iota(square, 0), same, 0), axis=1, keepdims=True)
    place = jnp.minimum(CAP * jnp.bitwise_xor(owner_dev, me) + rank_row, CAP * n - 1)
    place = jnp.concatenate([place, jnp.zeros((1, pts - blocks), jnp.int32)], axis=1)
    elem_col = own_col - dev_col * elems
    lane_of = jnp.where(rank_col < CAP, jnp.bitwise_xor(dev_col, me) + n * rank_col, -1)
    for r in range(wide):
        here_lane = iota((blocks, lanes), 1) + lanes * r == lane_of
        row = jnp.sum(jnp.where(here_lane, elem_col, 0), axis=0, keepdims=True)
        idsend[r:r + 1, :] = row
        idrecv[r:r + 1, :] = row
    slotv[...] = place
    slot_copy = pltpu.make_async_copy(slotv, slots, slotsem)
    slot_copy.start()

    pl.semaphore_wait(barrier, n - 1)
    def send_points(k):
        g = k // group_peers
        pltpu.make_async_remote_copy(
            src_ref=idsend, dst_ref=idrecv.at[pl.ds(wide * k, wide), :], send_sem=s0, recv_sem=r0.at[g],
            device_id=peer(k), device_id_type=pl.DeviceIdType.MESH).start()
        pltpu.make_async_remote_copy(
            src_ref=send.at[message(k), :], dst_ref=recv.at[message(k), :], send_sem=s1, recv_sem=r1.at[g],
            device_id=peer(k), device_id_type=pl.DeviceIdType.MESH).start()

    for_peers(1, n, send_points)

    row, col = iota((24, 24), 0), iota((24, 24), 1)
    both_bits = jnp.bitwise_and(row, col) % 8
    odd = (both_bits + both_bits // 2 + both_bits // 4) % 2
    hada = jnp.where(row // 8 == col // 8, (1 - 2 * odd).astype(F32) * 0.125, 0.0)
    get_shift.wait()
    bits = row % 8
    sign = (1 - 2 * ((bits + bits // 2 + bits // 4) % 2)).astype(F32)
    coefs = jnp.dot(hada * sign, shift_ref[...], precision=EXACT, preferred_element_type=F32)
    c_hi = coefs.astype(BF16)
    rest = coefs - c_hi.astype(F32)
    c_mid = rest.astype(BF16)
    c_lo = (rest - c_mid.astype(F32)).astype(BF16)

    fetch.wait()
    low_sub = iota((8, 128), 0) < 4
    low_lane = iota((8, 128), 1) < 64
    keep = low_sub == low_lane

    def split(e, carry):
        parts = []
        for q in range(4):
            x = fbuf[e, :, q * 128:(q + 1) * 128]
            x = jnp.concatenate([x, x], axis=0)
            hi = x.astype(BF16).astype(F32)
            lo = x - hi
            a = jnp.where(low_sub, hi, lo)
            b = pltpu.roll(jnp.where(low_sub, lo, hi), 64, axis=1)
            parts.append(jnp.where(keep, a, b))
        table[e] = jnp.concatenate(parts, axis=0).astype(BF16)
        return carry

    lax.fori_loop(0, elems, split, 0, unroll=4)

    per = group_peers
    count = CAP * per

    def run_group(g, first):
        base = g * per
        got = per - 1 if first else per
        start = base + 1 if first else base
        for_wait(start, got, recv, r1.at[g])

        def gather(a):
            return jnp.concatenate(
                [recv[pl.ds(8 * base + 3 * c + a, per, stride=8), :] for c in range(CAP)], axis=0)

        y = [gather(a) for a in range(3)]
        taken = idrecv.at[pl.ds(wide * start, wide * got), :]
        pltpu.make_async_copy(taken, taken, r0.at[g]).wait()
        id_copy = pltpu.make_async_copy(idrecv.at[pl.ds(wide * base, wide * per), :], ids.at[pl.ds(wide * base, wide * per), :], idsem)
        id_copy.start()
        id_lane = iota((per, lanes), 1) - iota((per, lanes), 0)
        id_cols = []
        for c in range(CAP):
            at = c * n + base
            id_rows = idrecv[pl.ds(wide * base + at // lanes, per, stride=wide), :]
            id_cols.append(jnp.sum(jnp.where(id_lane == at % lanes, id_rows, 0), axis=1, keepdims=True))
        elem = jnp.concatenate(id_cols, axis=0)
        pick = jnp.where(elem == iota((count, elems), 1), 1.0, 0.0).astype(BF16)
        chosen = sum(lax.dot_general(pick, c, NT, preferred_element_type=F32) for c in (c_hi, c_mid, c_lo))
        coef = []
        for a in range(3):
            line = []
            for m in range(8):
                value = chosen[:, 8 * a + m:8 * a + m + 1]
                if m == 4 >> a:
                    value = value + 1.0
                line.append(jnp.broadcast_to(value, (count, pts)))
            coef.append(line)
        xi = newton(coef, y)
        for a in range(3):
            for i, value in enumerate(lagrange(xi[a])):
                lag[a, pl.ds(i, count, stride=8), :] = value
        id_copy.wait()
        for s in range(count):
            c, p = s // per, s % per
            e = ids[wide * (base + p) + (c * n + base) // lanes, (c * n + base) % lanes + p]
            left = table[e]
            lz = lag[2, 8 * s:8 * s + 8, :]
            w = jnp.concatenate([lag[1, 8 * s + j:8 * s + j + 1, :] * lz for j in range(8)], axis=0)
            w_hi = w.astype(BF16)
            w_lo = (w - w_hi.astype(F32)).astype(BF16)
            prod = jnp.dot(
                jnp.concatenate([left, left], axis=1),
                jnp.concatenate([w_hi, w_hi, w_lo, w_lo], axis=0),
                preferred_element_type=F32)
            total = None
            for q in range(4):
                lx = jnp.where(low_sub, lag[0, 8 * s + 2 * q:8 * s + 2 * q + 1, :],
                               lag[0, 8 * s + 2 * q + 1:8 * s + 2 * q + 2, :])
                term = prod[8 * q:8 * q + 8] * lx
                total = term if total is None else total + term
            total = total[0:4] + total[4:8]
            if first and p == 0:
                ret[c] = total
            else:
                res[CAP * (base + p) + c] = total
        for_peers_in = range(1 if first else 0, per)
        for p in for_peers_in:
            send_result(base + p, g).start()

    run_group(0, True)
    if unrolled:
        for g in range(1, groups):
            run_group(g, False)
    else:
        lax.fori_loop(1, groups, lambda g, c: (run_group(g, False), c)[1], 0)

    slot_copy.wait()
    for g in range(groups):
        start, got = (1, per - 1) if g == 0 else (g * per, per)
        back = ret.at[pl.ds(CAP * start, CAP * got)]
        pltpu.make_async_copy(back, back, r2.at[g]).wait()
    for b in range(blocks):
        out_ref[b] = ret[slots[0, b]]
    rest_ids = idrecv.at[pl.ds(wide, wide * (n - 1)), :]
    pltpu.make_async_copy(rest_ids, rest_ids, s0).wait()
    for_wait(1, n - 1, send, s1)
    left = res.at[pl.ds(CAP, CAP * (n - 1))]
    pltpu.make_async_copy(left, left, s2).wait()


def shards(sizes, old_fields, corner_shift, targets, owners):
    n = sizes[0] * sizes[1] * sizes[2]
    elems, nvar, nodes = old_fields.shape
    blocks = owners.shape[0]
    pts = targets.shape[1] // blocks
    assert n & (n - 1) == 0 and elems & (elems - 1) == 0 and nvar == 4 and nodes == 512
    group_peers = min(GROUP_PEERS, n)
    groups = n // group_peers
    wide = (CAP * n + 127) // 128
    points = targets.reshape(3, blocks, pts).transpose(1, 0, 2)
    vmem = pl.BlockSpec(memory_space=pltpu.VMEM)
    hbm = pl.BlockSpec(memory_space=pltpu.HBM)
    message = pltpu.VMEM((8 * n, pts), F32)
    result = pltpu.VMEM((CAP * n, nvar, pts), F32)
    out = pl.pallas_call(
        functools.partial(kernel, sizes, group_peers),
        out_shape=jax.ShapeDtypeStruct((blocks, nvar, pts), F32),
        in_specs=[hbm] * 4,
        out_specs=vmem,
        scratch_shapes=[
            pltpu.VMEM((1, blocks), jnp.int32),
            pltpu.VMEM((blocks, 3, pts), F32),
            pltpu.VMEM((24, elems), F32),
            pltpu.VMEM((elems, nvar, nodes), F32),
            pltpu.VMEM((elems, 32, 128), BF16),
            message, message, result, result,
            pltpu.VMEM((3, 8 * CAP * group_peers, pts), F32),
            pltpu.VMEM((wide, 128), jnp.int32),
            pltpu.VMEM((wide * n, 128), jnp.int32),
            pltpu.SMEM((wide * n, 128), jnp.int32),
            pltpu.VMEM((1, pts), jnp.int32),
            pltpu.SMEM((1, pts), jnp.int32),
            *[pltpu.SemaphoreType.DMA] * 6,
            pltpu.SemaphoreType.DMA, pltpu.SemaphoreType.DMA((groups,)),
            pltpu.SemaphoreType.DMA, pltpu.SemaphoreType.DMA((groups,)),
            pltpu.SemaphoreType.DMA, pltpu.SemaphoreType.DMA((groups,)),
        ],
        compiler_params=pltpu.CompilerParams(
            collective_id=0, has_side_effects=True, vmem_limit_bytes=16 * 1024 * 1024),
    )(*[pltpu.with_memory_space_constraint(x, pltpu.HBM) for x in (owners.reshape(1, blocks), points, corner_shift, old_fields)])
    return out.transpose(1, 0, 2).reshape(nvar, blocks * pts)


def solution(mesh):
    sizes = tuple(mesh.shape[a] for a in AXES)
    in_specs = (
        P(("groups", "block", "seg", "sub"), None, None),
        P(None, ("groups", "block", "seg", "sub")),
        P(None, ("groups", "block", "seg", "sub")),
        P(("groups", "block", "seg", "sub")),
    )
    out_specs = P(None, ("groups", "block", "seg", "sub"))
    return jax.shard_map(functools.partial(shards, sizes), mesh=mesh, in_specs=in_specs,
                         out_specs=out_specs, check_vma=False)
```

profile of v0, /device:TPU:0, one launch (start us, length us, event | category | flops | bytes accessed | tf_op | source)
XLA Modules:
  0.0 15.8 jit_solution(11651700092332825014)
XLA Ops:
  0.0 15.1 %shard_map.46 = f32[32,4,128]{2,1,0:T(4,128)S(1)} custom-call(s32[1,32]{1,0:T(1,128)} %bitcast.9, f32[32,3,128]{2,1,0:T(4,128)} %bitcast.8, f32[24,64]{1,0:T(8,128)} %shift_hbm.1, f32[64,4,512]{2,1,0:T(4,128)} %fields_hbm.1), custom_call_target="tpu_custom_call" | custom-call | tf_op jit(solution)/shard_map/pallas_call | solution.py:344
  15.1 0.6 %copy.6 = f32[4,4096]{1,0:T(4,128)} copy(f32[4,4096]{1,0:T(4,128)S(1)} %bitcast.7) | data formatting | bytes 131072
where the time goes:
time: 15.9 us; the launch traced here: 15.8 us
  Pallas kernels  15.1 us (95%)
  local copies, waits for them, and re-layouts  0.63 us (4%)
    pallas_call x1, Pallas kernels, shards(): pl.pallas_call(functools.partial(kernel, sizes, group_peers), out_shape=j...  15.1 us
    unnamed x1, local copies, waits for them, and re-layouts  0.63 us

commit v1 on v0

--- a/solution.py
+++ b/solution.py
@@ -327,6 +327,241 @@
     pltpu.make_async_copy(left, left, s2).wait()
 
 
+def pair_kernel(sizes, owners_hbm, targets_hbm, shift_hbm, fields_hbm, out_ref,
+                owners_ref, targets_ref, shift_ref, fbuf, ctab, send, give, recv, cbuf, lag, res, ret, slots,
+                osem, tsem, csem, fsem, s_rel, r_rel, s_fld, r_fld, s_shf, r_shf, s1, r1, s2, r2):
+    nb, ns, nc = sizes
+    half = nb * ns // 2
+    blocks = owners_ref.shape[1]
+    elems = shift_ref.shape[2]
+    pts = out_ref.shape[2]
+    quad = nc * CAP
+    rows = 4 * quad
+    per = 2 * quad
+    b, s, c = [lax.axis_index(a) for a in AXES]
+    chip = b * ns + s
+    other = 1 - c
+    top = nb // 2
+    across = b + c * top * (1 - 2 * ((b // top) % 2))
+
+    def peer(j, core):
+        return {"block": flip(across, j // ns), "seg": flip(s, j % ns), "sub": core}
+
+    def unless_here(j, body):
+        if j == 0:
+            pl.when(c == 1)(body)
+        else:
+            body()
+
+    def remote(src, dst, send_sem, recv_sem, device):
+        return pltpu.make_async_remote_copy(
+            src_ref=src, dst_ref=dst, send_sem=send_sem, recv_sem=recv_sem,
+            device_id=device, device_id_type=pl.DeviceIdType.MESH)
+
+    def wait_for(part, sem):
+        pltpu.make_async_copy(part, part, sem).wait()
+
+    get_owners = pltpu.make_async_copy(owners_hbm, owners_ref, osem)
+    get_owners.start()
+    get_targets = pltpu.make_async_copy(targets_hbm, targets_ref, tsem)
+    get_targets.start()
+    barrier = pltpu.get_barrier_semaphore()
+
+    def hello(device):
+        pl.semaphore_signal(barrier, inc=1, device_id=device, device_id_type=pl.DeviceIdType.MESH)
+
+    for j in reversed(range(half)):
+        unless_here(j, lambda: hello(peer(j, c)))
+    sibling = {"block": b, "seg": s, "sub": other}
+    hello(sibling)
+    get_shift = pltpu.make_async_copy(shift_hbm, shift_ref.at[0], csem)
+    get_shift.start()
+    fetch = pltpu.make_async_copy(fields_hbm, fbuf.at[pl.ds(0, elems)], fsem)
+    fetch.start()
+
+    shift_bits = elems.bit_length() - 1
+    square = (blocks, blocks)
+    get_owners.wait()
+    own = owners_ref[...]
+    own_rows = jnp.broadcast_to(own, square)
+    diag = iota(square, 0) == iota(square, 1)
+    own_col = jnp.sum(jnp.where(diag, own_rows, 0), axis=1, keepdims=True)
+    dev_col = jnp.right_shift(own_col, shift_bits)
+    dev_row = jnp.right_shift(own_rows, shift_bits)
+    same = jnp.where(dev_col == dev_row, 1, 0)
+    rank_row = jnp.sum(jnp.where(iota(square, 0) < iota(square, 1), same, 0), axis=0, keepdims=True)
+    rank_col = jnp.sum(jnp.where(iota(square, 1) < iota(square, 0), same, 0), axis=1, keepdims=True)
+    base_chip = jnp.bitwise_xor(chip, c * half)
+
+    def slot_of(dev, rank):
+        rel = jnp.bitwise_xor(jnp.right_shift(dev, 1), base_chip)
+        return rel, (rel * nc + jnp.bitwise_and(dev, 1)) * CAP + rank
+
+    rel_col, slot_col = slot_of(dev_col, rank_col)
+    turned = jnp.where(rel_col >= half, 1, 0)
+    side = jnp.bitwise_xor(jnp.bitwise_xor(jnp.bitwise_and(dev_col, 1), c), turned)
+    elem_col = own_col - dev_col * elems + elems * side
+    _, slot_row = slot_of(jnp.right_shift(own, shift_bits), rank_row)
+    count = 2 * half * quad
+    pick = jnp.where(iota((count, blocks), 0) == slot_row, 1.0, 0.0)
+    id_rows = jnp.broadcast_to(elem_col.astype(F32), (blocks, pts))
+    get_targets.wait()
+    cat = jnp.concatenate([targets_ref[:, a, :] for a in range(3)] + [id_rows], axis=1)
+    packed = jnp.dot(pick, cat, precision=EXACT, preferred_element_type=F32)
+    for a in range(4):
+        for j in range(half):
+            send[j, pl.ds(a, quad, stride=4), :] = packed[quad * j:quad * (j + 1), a * pts:(a + 1) * pts]
+            give[j, pl.ds(a, quad, stride=4), :] = packed[quad * (half + j):quad * (half + j + 1), a * pts:(a + 1) * pts]
+    slot_safe = jnp.minimum(jnp.maximum(slot_col, 0), count - 1)
+    for k in range(blocks):
+        slots[0, k] = slot_safe[k, 0]
+
+    low_sub = iota((8, 128), 0) < 4
+    low_lane = iota((8, 128), 1) < 64
+
+    def split(e):
+        parts = []
+        for r in range(0, fbuf.shape[1], 8):
+            x = fbuf[e, r:r + 8, :]
+            hi = x.astype(BF16).astype(F32)
+            lo = x - hi
+            turned = pltpu.roll(jnp.where(low_lane, lo, hi), 64, axis=1)
+            parts += [jnp.where(low_lane, hi, turned), jnp.where(low_lane, turned, lo)]
+        return jnp.concatenate(parts, axis=0).astype(BF16)
+
+    row, col = iota((24, 24), 0), iota((24, 24), 1)
+    both_bits = jnp.bitwise_and(row, col) % 8
+    odd = (both_bits + both_bits // 2 + both_bits // 4) % 2
+    hada = jnp.where(row // 8 == col // 8, (1 - 2 * odd).astype(F32) * 0.125, 0.0)
+    bits = row % 8
+    sign = (1 - 2 * ((bits + bits // 2 + bits // 4) % 2)).astype(F32)
+    line = iota((24, elems), 0)
+    unit = jnp.where(line % 8 == jnp.right_shift(4, line // 8), 1.0, 0.0)
+
+    def spread(side):
+        coefs = jnp.dot(hada * sign, shift_ref[side], precision=EXACT, preferred_element_type=F32) + unit
+        for e in range(elems):
+            ctab[side * elems + e] = jnp.broadcast_to(coefs[:, e:e + 1], (24, pts))
+
+    get_shift.wait()
+    fetch.wait()
+    pl.semaphore_wait(barrier, half + c)
+    theirs = send.at[:, pl.ds(rows, rows), :]
+    remote(give, theirs, s_rel, r_rel, sibling).start()
+    wait_for(theirs, r_rel)
+    for j in reversed(range(half)):
+        unless_here(j, lambda: remote(
+            send.at[j], recv.at[pl.ds(2 * rows * j, 2 * rows), :], s1, r1.at[j], peer(j, c)).start())
+    remote(shift_ref.at[0], shift_ref.at[1], s_shf, r_shf, sibling).start()
+    remote(fbuf.at[pl.ds(0, elems)], fbuf.at[pl.ds(elems, elems)], s_fld, r_fld, sibling).start()
+
+    @pl.when(c == 0)
+    def _():
+        recv[0:2 * rows, :] = send[0]
+
+    spread(0)
+    wait_for(shift_ref.at[1], r_shf)
+    spread(1)
+    wait_for(fbuf.at[pl.ds(elems, elems)], r_fld)
+
+    for j in range(half):
+        base = 2 * rows * j
+        unless_here(j, lambda: wait_for(recv.at[pl.ds(base, 2 * rows), :], r1.at[j]))
+        y = [recv[pl.ds(base + a, per, stride=4), :] for a in range(3)]
+        ids = recv[pl.ds(base + 3, per, stride=4), :].astype(jnp.int32)
+        ids = jnp.minimum(jnp.maximum(ids, 0), 2 * elems - 1)
+        elem = [ids[k, 0] for k in range(per)]
+        for k in range(per):
+            for a in range(3):
+                cbuf[a, 8 * k:8 * k + 8, :] = ctab[elem[k], 8 * a:8 * a + 8, :]
+        coef = [[cbuf[a, pl.ds(m, per, stride=8), :] for m in range(8)] for a in range(3)]
+        xi = newton(coef, y)
+        for a in range(3):
+            for i, value in enumerate(lagrange(xi[a])):
+                lag[a, pl.ds(i, per, stride=8), :] = value
+        for k in range(per):
+            left = split(elem[k])
+            lz = lag[2, 8 * k:8 * k + 8, :]
+            w = jnp.concatenate([lag[1, 8 * k + i:8 * k + i + 1, :] * lz for i in range(8)], axis=0)
+            w_hi = w.astype(BF16)
+            w_lo = (w - w_hi.astype(F32)).astype(BF16)
+            prod = jnp.dot(
+                jnp.concatenate([left, left], axis=1),
+                jnp.concatenate([w_hi, w_hi, w_lo, w_lo], axis=0),
+                preferred_element_type=F32)
+            total = None
+            for q in range(4):
+                i = 8 * k + 4 * (q // 2) + q % 2
+                lx = jnp.where(low_sub, lag[0, i:i + 1, :], lag[0, i + 2:i + 3, :])
+                term = prod[8 * q:8 * q + 8] * lx
+                total = term if total is None else total + term
+            res[per * j + k] = total[0:4] + total[4:8]
+
+        def result(part, core, slot):
+            return remote(res.at[pl.ds(per * j + quad * part, quad)], ret.at[pl.ds(quad * slot, quad)],
+                          s2, r2.at[slot], peer(j, core))
+
+        result(1, other, half + j).start()
+        unless_here(j, lambda: result(0, c, j).start())
+        if j == 0:
+            @pl.when(c == 0)
+            def _():
+                ret[0:quad] = res[0:quad]
+
+    for g in range(2 * half):
+        unless_here(g, lambda: wait_for(ret.at[pl.ds(quad * g, quad)], r2.at[g]))
+    for k in range(blocks):
+        out_ref[k] = ret[slots[0, k]]
+    wait_for(theirs, s_rel)
+    wait_for(shift_ref.at[1], s_shf)
+    wait_for(fbuf.at[pl.ds(elems, elems)], s_fld)
+
+    def finish(skip):
+        wait_for(recv.at[pl.ds(2 * rows * skip, 2 * rows * (half - skip)), :], s1)
+        wait_for(ret.at[pl.ds(quad * skip, quad * (2 * half - skip))], s2)
+
+    pl.when(c == 0)(lambda: finish(1))
+    pl.when(c == 1)(lambda: finish(0))
+
+
+def paired(sizes, old_fields, corner_shift, points, owners):
+    half = sizes[0] * sizes[1] // 2
+    elems, nvar, nodes = old_fields.shape
+    blocks, _, pts = points.shape
+    quad = sizes[2] * CAP
+    rows = 4 * quad
+    fields = old_fields.reshape(elems, nvar, nodes // 128, 128).transpose(0, 2, 1, 3)
+    fields = fields.reshape(elems, nvar * nodes // 128, 128)
+    vmem = pl.BlockSpec(memory_space=pltpu.VMEM)
+    hbm = pl.BlockSpec(memory_space=pltpu.HBM)
+    result = pltpu.VMEM((2 * half * quad, nvar, pts), F32)
+    dma = pltpu.SemaphoreType.DMA
+    return pl.pallas_call(
+        functools.partial(pair_kernel, sizes),
+        out_shape=jax.ShapeDtypeStruct((blocks, nvar, pts), F32),
+        in_specs=[hbm] * 4,
+        out_specs=vmem,
+        scratch_shapes=[
+            pltpu.VMEM((1, blocks), jnp.int32),
+            pltpu.VMEM((blocks, 3, pts), F32),
+            pltpu.VMEM((2, 24, elems), F32),
+            pltpu.VMEM((2 * elems, nvar * nodes // 128, 128), F32),
+            pltpu.VMEM((2 * elems, 24, pts), F32),
+            pltpu.VMEM((half, 2 * rows, pts), F32),
+            pltpu.VMEM((half, rows, pts), F32),
+            pltpu.VMEM((2 * rows * half, pts), F32),
+            pltpu.VMEM((3, 16 * quad, pts), F32),
+            pltpu.VMEM((3, 16 * quad, pts), F32),
+            result, result,
+            pltpu.SMEM((1, blocks), jnp.int32),
+            *[dma] * 4, *[dma] * 6,
+            dma, dma((half,)), dma, dma((2 * half,)),
+        ],
+        compiler_params=pltpu.CompilerParams(
+            collective_id=0, has_side_effects=True, vmem_limit_bytes=24 * 1024 * 1024),
+    )(*[pltpu.with_memory_space_constraint(x, pltpu.HBM) for x in (owners.reshape(1, blocks), points, corner_shift, fields)])
+
+
 def shards(sizes, old_fields, corner_shift, targets, owners):
     n = sizes[0] * sizes[1] * sizes[2]
     elems, nvar, nodes = old_fields.shape
@@ -337,6 +572,9 @@
     groups = n // group_peers
     wide = (CAP * n + 127) // 128
     points = targets.reshape(3, blocks, pts).transpose(1, 0, 2)
+    if n <= 32 and sizes[0] > 1 and sizes[2] == 2:
+        out = paired(sizes, old_fields, corner_shift, points, owners)
+        return out.transpose(1, 0, 2).reshape(nvar, blocks * pts)
     vmem = pl.BlockSpec(memory_space=pltpu.VMEM)
     hbm = pl.BlockSpec(memory_space=pltpu.HBM)
     message = pltpu.VMEM((8 * n, pts), F32)

time: 15.9 us -> 14.1 us (0.89)
  Pallas kernels: 15.1 us -> 13.3 us
    pallas_call x1, Pallas kernels: 15.1 us -> 13.3 us  [paired(): pl.pallas_call(functools.partial(pair_kernel, sizes), out_shape=jax.Shape...]
where the time goes in v1:
time: 14.1 us; the launch traced here: 14 us
  Pallas kernels  13.3 us (94%)
  local copies, waits for them, and re-layouts  0.63 us (4%)
    pallas_call x1, Pallas kernels, paired(): pl.pallas_call(functools.partial(pair_kernel, sizes), out_shape=jax.Shape...  13.3 us
    unnamed x1, local copies, waits for them, and re-layouts  0.63 us

profile of v1, /device:TPU:0, one launch (start us, length us, event | category | flops | bytes accessed | tf_op | source)
XLA Modules:
  0.0 14.0 jit_solution(1349598666020703761)
XLA Ops:
  0.0 13.3 %shard_map.46 = f32[32,4,128]{2,1,0:T(4,128)S(1)} custom-call(s32[1,32]{1,0:T(1,128)} %bitcast.15, f32[32,3,128]{2,1,0:T(4,128)} %bitcast.14, f32[24,64]{1,0:T(8,128)} %shift_hbm.1, f32[64,16,128]{2,1,0:T(8,128)} %bitcast.13), custom_call_target="tpu_custom_call" | custom-call | tf_op jit(solution)/shard_map/pallas_call | solution.py:539
  13.3 0.6 %copy.7 = f32[4,4096]{1,0:T(4,128)} copy(f32[4,4096]{1,0:T(4,128)S(1)} %bitcast.12) | data formatting | bytes 131072

commit v2 on v1

--- a/solution.py
+++ b/solution.py
@@ -347,6 +347,9 @@
     def peer(j, core):
         return {"block": flip(across, j // ns), "seg": flip(s, j % ns), "sub": core}
 
+    def near(j, core):
+        return {"block": flip(b, j // ns), "seg": flip(s, j % ns), "sub": core}
+
     def unless_here(j, body):
         if j == 0:
             pl.when(c == 1)(body)
@@ -374,6 +377,12 @@
         unless_here(j, lambda: hello(peer(j, c)))
     sibling = {"block": b, "seg": s, "sub": other}
     hello(sibling)
+
+    @pl.when(c == 0)
+    def _():
+        for j in range(1, half):
+            hello(near(j, 1))
+
     get_shift = pltpu.make_async_copy(shift_hbm, shift_ref.at[0], csem)
     get_shift.start()
     fetch = pltpu.make_async_copy(fields_hbm, fbuf.at[pl.ds(0, elems)], fsem)
@@ -445,28 +454,46 @@
 
     get_shift.wait()
     fetch.wait()
-    pl.semaphore_wait(barrier, half + c)
+    pl.semaphore_wait(barrier, half + c * half)
     theirs = send.at[:, pl.ds(rows, rows), :]
-    remote(give, theirs, s_rel, r_rel, sibling).start()
-    wait_for(theirs, r_rel)
-    for j in reversed(range(half)):
-        unless_here(j, lambda: remote(
-            send.at[j], recv.at[pl.ds(2 * rows * j, 2 * rows), :], s1, r1.at[j], peer(j, c)).start())
+
+    @pl.when(c == 0)
+    def _():
+        remote(give, theirs, s_rel, r_rel, sibling).start()
+        for j in reversed(range(1, half)):
+            remote(send.at[j, pl.ds(0, rows), :], recv.at[pl.ds(2 * rows * j, rows), :], s1, r1.at[j], near(j, 0)).start()
+
+    @pl.when(c == 1)
+    def _():
+        def far(j):
+            remote(send.at[j], recv.at[pl.ds(2 * rows * j, 2 * rows), :], s1, r1.at[j], peer(j, 1)).start()
+
+        wait_for(theirs, r_rel)
+        for j in reversed(range(half // 2, half)):
+            far(j)
+        for j in reversed(range(half)):
+            remote(give.at[j], recv.at[pl.ds(2 * rows * j + rows, rows), :], s_rel, r1.at[j], near(j, 0)).start()
+        for j in reversed(range(half // 2)):
+            far(j)
+
     remote(shift_ref.at[0], shift_ref.at[1], s_shf, r_shf, sibling).start()
     remote(fbuf.at[pl.ds(0, elems)], fbuf.at[pl.ds(elems, elems)], s_fld, r_fld, sibling).start()
 
     @pl.when(c == 0)
     def _():
-        recv[0:2 * rows, :] = send[0]
+        recv[0:rows, :] = send[0, 0:rows, :]
 
     spread(0)
     wait_for(shift_ref.at[1], r_shf)
     spread(1)
     wait_for(fbuf.at[pl.ds(elems, elems)], r_fld)
 
-    for j in range(half):
+    order = list(range(half - 2)) + [half - 1, half - 2] if half > 1 else [0]
+    for j in order:
         base = 2 * rows * j
         unless_here(j, lambda: wait_for(recv.at[pl.ds(base, 2 * rows), :], r1.at[j]))
+        if j == 0:
+            pl.when(c == 0)(lambda: wait_for(recv.at[pl.ds(base + rows, rows), :], r1.at[j]))
         y = [recv[pl.ds(base + a, per, stride=4), :] for a in range(3)]
         ids = recv[pl.ds(base + 3, per, stride=4), :].astype(jnp.int32)
         ids = jnp.minimum(jnp.maximum(ids, 0), 2 * elems - 1)
@@ -512,12 +539,12 @@
         unless_here(g, lambda: wait_for(ret.at[pl.ds(quad * g, quad)], r2.at[g]))
     for k in range(blocks):
         out_ref[k] = ret[slots[0, k]]
-    wait_for(theirs, s_rel)
+    wait_for(give, s_rel)
     wait_for(shift_ref.at[1], s_shf)
     wait_for(fbuf.at[pl.ds(elems, elems)], s_fld)
 
     def finish(skip):
-        wait_for(recv.at[pl.ds(2 * rows * skip, 2 * rows * (half - skip)), :], s1)
+        wait_for(recv.at[pl.ds(0, (half - 1 if skip else 2 * half) * rows), :], s1)
         wait_for(ret.at[pl.ds(quad * skip, quad * (2 * half - skip))], s2)
 
     pl.when(c == 0)(lambda: finish(1))

time: 14.1 us -> 13.5 us (0.957)
  Pallas kernels: 13.3 us -> 12.7 us
    pallas_call x1, Pallas kernels: 13.3 us -> 12.7 us  [paired(): pl.pallas_call(functools.partial(pair_kernel, sizes), out_shape=jax.Shape...]
where the time goes in v2:
time: 13.5 us; the launch traced here: 13.3 us
  Pallas kernels  12.7 us (94%)
  local copies, waits for them, and re-layouts  0.63 us (5%)
    pallas_call x1, Pallas kernels, paired(): pl.pallas_call(functools.partial(pair_kernel, sizes), out_shape=jax.Shape...  12.7 us
    unnamed x1, local copies, waits for them, and re-layouts  0.63 us

profile of v2, /device:TPU:0, one launch (start us, length us, event | category | flops | bytes accessed | tf_op | source)
XLA Modules:
  0.0 13.3 jit_solution(4655367727461930133)
XLA Ops:
  0.0 12.7 %shard_map.46 = f32[32,4,128]{2,1,0:T(4,128)S(1)} custom-call(s32[1,32]{1,0:T(1,128)} %bitcast.15, f32[32,3,128]{2,1,0:T(4,128)} %bitcast.14, f32[24,64]{1,0:T(8,128)} %shift_hbm.1, f32[64,16,128]{2,1,0:T(8,128)} %bitcast.13), custom_call_target="tpu_custom_call" | custom-call | tf_op jit(solution)/shard_map/pallas_call | solution.py:566
  12.7 0.6 %copy.7 = f32[4,4096]{1,0:T(4,128)} copy(f32[4,4096]{1,0:T(4,128)S(1)} %bitcast.12) | data formatting | bytes 131072

commit v3 on v1

--- a/solution.py
+++ b/solution.py
@@ -328,8 +328,8 @@
 
 
 def pair_kernel(sizes, owners_hbm, targets_hbm, shift_hbm, fields_hbm, out_ref,
-                owners_ref, targets_ref, shift_ref, fbuf, ctab, send, give, recv, cbuf, lag, res, ret, slots,
-                osem, tsem, csem, fsem, s_rel, r_rel, s_fld, r_fld, s_shf, r_shf, s1, r1, s2, r2):
+                owners_ref, targets_ref, shift_ref, fbuf, ctab, send, give, via, recv, cbuf, lag, res, ret, slots,
+                osem, tsem, csem, fsem, s_rel, r_rel, s_fld, r_fld, s_shf, r_shf, s1, r1, s2, r2, r_via, here):
     nb, ns, nc = sizes
     half = nb * ns // 2
     blocks = owners_ref.shape[1]
@@ -347,6 +347,9 @@
     def peer(j, core):
         return {"block": flip(across, j // ns), "seg": flip(s, j % ns), "sub": core}
 
+    def near(j, core):
+        return {"block": flip(b, j // ns), "seg": flip(s, j % ns), "sub": core}
+
     def unless_here(j, body):
         if j == 0:
             pl.when(c == 1)(body)
@@ -370,14 +373,55 @@
     def hello(device):
         pl.semaphore_signal(barrier, inc=1, device_id=device, device_id_type=pl.DeviceIdType.MESH)
 
-    for j in reversed(range(half)):
-        unless_here(j, lambda: hello(peer(j, c)))
     sibling = {"block": b, "seg": s, "sub": other}
-    hello(sibling)
+    partner = {"block": b, "seg": flip(s, 1), "sub": 1}
+    first = jnp.logical_and(c == 1, b == 0)
+    high = jnp.logical_and(c == 1, b >= top)
+
+    def above(j):
+        return b % 2 == 0 if j // ns else s == 0
+
+    def below(j):
+        return b % 2 == 1 if j // ns else s == 1
+
+    @pl.when(c == 1)
+    def _():
+        @pl.when(b < top)
+        def _():
+            for j in reversed(range(half)):
+                hello(peer(j, 1))
+
+        pl.when(b == 0)(lambda: hello(partner))
+        hello(sibling)
+
+    @pl.when(c == 0)
+    def _():
+        for j in reversed(range(1, half)):
+            pl.when(above(j))(lambda: hello(near(j, 0)))
+
     get_shift = pltpu.make_async_copy(shift_hbm, shift_ref.at[0], csem)
     get_shift.start()
     fetch = pltpu.make_async_copy(fields_hbm, fbuf.at[pl.ds(0, elems)], fsem)
     fetch.start()
+
+    pl.when(c == 0)(lambda: pl.semaphore_wait(barrier, 1 + (b % 2) * ns + s))
+    pl.when(high)(lambda: pl.semaphore_wait(barrier, half))
+
+    def answer(j, device):
+        pl.semaphore_signal(here.at[j], inc=1, device_id=device, device_id_type=pl.DeviceIdType.MESH)
+
+    @pl.when(high)
+    def _():
+        for j in reversed(range(half)):
+            if j % ns:
+                pl.when(flip(across, j // ns) != 0)(lambda: answer(j, peer(j, 1)))
+            else:
+                answer(j, peer(j, 1))
+
+    @pl.when(c == 0)
+    def _():
+        for j in reversed(range(1, half)):
+            pl.when(below(j))(lambda: answer(j, near(j, 0)))
 
     shift_bits = elems.bit_length() - 1
     square = (blocks, blocks)
@@ -445,28 +489,90 @@
 
     get_shift.wait()
     fetch.wait()
-    pl.semaphore_wait(barrier, half + c)
+    pl.when(first)(lambda: pl.semaphore_wait(barrier, 1))
     theirs = send.at[:, pl.ds(rows, rows), :]
-    remote(give, theirs, s_rel, r_rel, sibling).start()
-    wait_for(theirs, r_rel)
-    for j in reversed(range(half)):
-        unless_here(j, lambda: remote(
-            send.at[j], recv.at[pl.ds(2 * rows * j, 2 * rows), :], s1, r1.at[j], peer(j, c)).start())
-    remote(shift_ref.at[0], shift_ref.at[1], s_shf, r_shf, sibling).start()
-    remote(fbuf.at[pl.ds(0, elems)], fbuf.at[pl.ds(elems, elems)], s_fld, r_fld, sibling).start()
+
+    def heard(j):
+        pl.semaphore_wait(here.at[j], 1)
+
+    def share():
+        remote(shift_ref.at[0], shift_ref.at[1], s_shf, r_shf, sibling).start()
+        remote(fbuf.at[pl.ds(0, elems)], fbuf.at[pl.ds(elems, elems)], s_fld, r_fld, sibling).start()
+
+    corner = (b % 2) * ns + s
+
+    def request(src, group, device):
+        at = pl.multiple_of(2 * rows * group, 2 * rows)
+        remote(src, recv.at[pl.ds(at, 2 * rows), :], s1, r1.at[group], device).start()
 
     @pl.when(c == 0)
     def _():
-        recv[0:2 * rows, :] = send[0]
+        remote(give, theirs, s_rel, r_rel, sibling).start()
+        share()
+        wait_for(theirs, r_rel)
+        for j in reversed(range(1, half)):
+            pl.when(above(j))(lambda: heard(j))
+            request(send.at[j], corner, near(j, 0))
+        recv[pl.ds(pl.multiple_of(2 * rows * corner, 2 * rows), 2 * rows), :] = send[0]
+
+    @pl.when(c == 1)
+    def _():
+        wait_for(theirs, r_rel)
+
+        @pl.when(b == 0)
+        def _():
+            for j in reversed(range(1, half, ns)):
+                remote(send.at[j], via.at[j // ns], s1, r_via.at[j // ns], partner).start()
+
+        remote(give, theirs, s_rel, r_rel, sibling).start()
+
+        def pass_on(i):
+            wait_for(via.at[i], r_via.at[i])
+            request(via.at[i], flip(s, 1), peer(ns * i, 1))
+
+        def own(i):
+            request(send.at[ns * i], corner, peer(ns * i, 1))
+
+        columns = list(reversed(range(half // ns)))
+
+        @pl.when(jnp.logical_and(b == 0, s == 0))
+        def _():
+            for i in columns:
+                heard(ns * i)
+                own(i)
+            share()
+            for i in columns:
+                pass_on(i)
+
+        @pl.when(jnp.logical_and(b == 0, s == 1))
+        def _():
+            for i in columns:
+                heard(ns * i)
+                pass_on(i)
+                own(i)
+            share()
+
+        @pl.when(b > 0)
+        def _():
+            for j in reversed(range(half)):
+                pl.when(b < top)(lambda: heard(j))
+                request(send.at[j], corner, peer(j, 1))
+            share()
 
     spread(0)
     wait_for(shift_ref.at[1], r_shf)
     spread(1)
     wait_for(fbuf.at[pl.ds(elems, elems)], r_fld)
 
-    for j in range(half):
-        base = 2 * rows * j
-        unless_here(j, lambda: wait_for(recv.at[pl.ds(base, 2 * rows), :], r1.at[j]))
+    for g in range(half):
+        base = 2 * rows * g
+        z, x = g // ns, g % ns
+        local = jnp.logical_and(c == 0, corner == g)
+
+        def unless_local(body):
+            pl.when(jnp.logical_not(local))(body)
+
+        unless_local(lambda: wait_for(recv.at[pl.ds(base, 2 * rows), :], r1.at[g]))
         y = [recv[pl.ds(base + a, per, stride=4), :] for a in range(3)]
         ids = recv[pl.ds(base + 3, per, stride=4), :].astype(jnp.int32)
         ids = jnp.minimum(jnp.maximum(ids, 0), 2 * elems - 1)
@@ -495,24 +601,26 @@
                 lx = jnp.where(low_sub, lag[0, i:i + 1, :], lag[0, i + 2:i + 3, :])
                 term = prod[8 * q:8 * q + 8] * lx
                 total = term if total is None else total + term
-            res[per * j + k] = total[0:4] + total[4:8]
-
-        def result(part, core, slot):
-            return remote(res.at[pl.ds(per * j + quad * part, quad)], ret.at[pl.ds(quad * slot, quad)],
-                          s2, r2.at[slot], peer(j, core))
-
-        result(1, other, half + j).start()
-        unless_here(j, lambda: result(0, c, j).start())
-        if j == 0:
-            @pl.when(c == 0)
-            def _():
-                ret[0:quad] = res[0:quad]
+            res[per * g + k] = total[0:4] + total[4:8]
+
+        slot = ns * flip(b % 2, z) + flip(s, x)
+
+        def result(part, core, to):
+            return remote(res.at[pl.ds(per * g + quad * part, quad)], ret.at[pl.ds(quad * to, quad)],
+                          s2, r2.at[to], {"block": 2 * (across // 2) + z, "seg": x, "sub": core})
+
+        result(1, other, half + slot).start()
+        unless_local(lambda: result(0, c, slot).start())
+
+        @pl.when(local)
+        def _():
+            ret[0:quad] = res[per * g:per * g + quad]
 
     for g in range(2 * half):
         unless_here(g, lambda: wait_for(ret.at[pl.ds(quad * g, quad)], r2.at[g]))
     for k in range(blocks):
         out_ref[k] = ret[slots[0, k]]
-    wait_for(theirs, s_rel)
+    wait_for(give, s_rel)
     wait_for(shift_ref.at[1], s_shf)
     wait_for(fbuf.at[pl.ds(elems, elems)], s_fld)
 
@@ -522,6 +630,7 @@
 
     pl.when(c == 0)(lambda: finish(1))
     pl.when(c == 1)(lambda: finish(0))
+    pl.when(first)(lambda: wait_for(via, s1))
 
 
 def paired(sizes, old_fields, corner_shift, points, owners):
@@ -549,6 +658,7 @@
             pltpu.VMEM((2 * elems, 24, pts), F32),
             pltpu.VMEM((half, 2 * rows, pts), F32),
             pltpu.VMEM((half, rows, pts), F32),
+            pltpu.VMEM((half // sizes[1], 2 * rows, pts), F32),
             pltpu.VMEM((2 * rows * half, pts), F32),
             pltpu.VMEM((3, 16 * quad, pts), F32),
             pltpu.VMEM((3, 16 * quad, pts), F32),
@@ -556,6 +666,7 @@
             pltpu.SMEM((1, blocks), jnp.int32),
             *[dma] * 4, *[dma] * 6,
             dma, dma((half,)), dma, dma((2 * half,)),
+            dma((half // sizes[1],)), pltpu.SemaphoreType.REGULAR((half,)),
         ],
         compiler_params=pltpu.CompilerParams(
             collective_id=0, has_side_effects=True, vmem_limit_bytes=24 * 1024 * 1024),
@@ -572,7 +683,7 @@
     groups = n // group_peers
     wide = (CAP * n + 127) // 128
     points = targets.reshape(3, blocks, pts).transpose(1, 0, 2)
-    if n <= 32 and sizes[0] > 1 and sizes[2] == 2:
+    if sizes[0] == 4 and sizes[1] == 2 and sizes[2] == 2:
         out = paired(sizes, old_fields, corner_shift, points, owners)
         return out.transpose(1, 0, 2).reshape(nvar, blocks * pts)
     vmem = pl.BlockSpec(memory_space=pltpu.VMEM)

time: 14.1 us -> 12.8 us (0.908)
  Pallas kernels: 13.3 us -> 12 us
    pallas_call x1, Pallas kernels: 13.3 us -> 12 us  [paired(): pl.pallas_call(functools.partial(pair_kernel, sizes), out_shape=jax.Shape...]
where the time goes in v3:
time: 12.8 us; the launch traced here: 12.6 us
  Pallas kernels  12 us (94%)
  local copies, waits for them, and re-layouts  0.63 us (5%)
    pallas_call x1, Pallas kernels, paired(): pl.pallas_call(functools.partial(pair_kernel, sizes), out_shape=jax.Shape...  12 us
    unnamed x1, local copies, waits for them, and re-layouts  0.63 us

profile of v3, /device:TPU:0, one launch (start us, length us, event | category | flops | bytes accessed | tf_op | source)
XLA Modules:
  0.0 12.6 jit_solution(13769890169820133878)
XLA Ops:
  0.0 12.0 %shard_map.46 = f32[32,4,128]{2,1,0:T(4,128)S(1)} custom-call(s32[1,32]{1,0:T(1,128)} %bitcast.15, f32[32,3,128]{2,1,0:T(4,128)} %bitcast.14, f32[24,64]{1,0:T(8,128)} %shift_hbm.1, f32[64,16,128]{2,1,0:T(8,128)} %bitcast.13), custom_call_target="tpu_custom_call" | custom-call | tf_op jit(solution)/shard_map/pallas_call | solution.py:648
  12.0 0.6 %copy.7 = f32[4,4096]{1,0:T(4,128)} copy(f32[4,4096]{1,0:T(4,128)S(1)} %bitcast.12) | data formatting | bytes 131072

commit v4 on v3

--- a/solution.py
+++ b/solution.py
@@ -329,7 +329,7 @@
 
 def pair_kernel(sizes, owners_hbm, targets_hbm, shift_hbm, fields_hbm, out_ref,
                 owners_ref, targets_ref, shift_ref, fbuf, ctab, send, give, via, recv, cbuf, lag, res, ret, slots,
-                osem, tsem, csem, fsem, s_rel, r_rel, s_fld, r_fld, s_shf, r_shf, s1, r1, s2, r2, r_via, here):
+                csem, fsem, sent, r_rel, r_shf, r_fld, r1, r2, r_via, here):
     nb, ns, nc = sizes
     half = nb * ns // 2
     blocks = owners_ref.shape[1]
@@ -364,9 +364,9 @@
     def wait_for(part, sem):
         pltpu.make_async_copy(part, part, sem).wait()
 
-    get_owners = pltpu.make_async_copy(owners_hbm, owners_ref, osem)
+    get_owners = pltpu.make_async_copy(owners_hbm, owners_ref, r2)
     get_owners.start()
-    get_targets = pltpu.make_async_copy(targets_hbm, targets_ref, tsem)
+    get_targets = pltpu.make_async_copy(targets_hbm, targets_ref, sent)
     get_targets.start()
     barrier = pltpu.get_barrier_semaphore()
 
@@ -496,18 +496,18 @@
         pl.semaphore_wait(here.at[j], 1)
 
     def share():
-        remote(shift_ref.at[0], shift_ref.at[1], s_shf, r_shf, sibling).start()
-        remote(fbuf.at[pl.ds(0, elems)], fbuf.at[pl.ds(elems, elems)], s_fld, r_fld, sibling).start()
+        remote(fbuf.at[pl.ds(0, elems)], fbuf.at[pl.ds(elems, elems)], sent, r_fld, sibling).start()
 
     corner = (b % 2) * ns + s
 
     def request(src, group, device):
         at = pl.multiple_of(2 * rows * group, 2 * rows)
-        remote(src, recv.at[pl.ds(at, 2 * rows), :], s1, r1.at[group], device).start()
+        remote(src, recv.at[pl.ds(at, 2 * rows), :], sent, r1.at[group], device).start()
 
     @pl.when(c == 0)
     def _():
-        remote(give, theirs, s_rel, r_rel, sibling).start()
+        remote(give, theirs, sent, r_rel, sibling).start()
+        remote(shift_ref.at[0], shift_ref.at[1], sent, r_shf, sibling).start()
         share()
         wait_for(theirs, r_rel)
         for j in reversed(range(1, half)):
@@ -522,9 +522,10 @@
         @pl.when(b == 0)
         def _():
             for j in reversed(range(1, half, ns)):
-                remote(send.at[j], via.at[j // ns], s1, r_via.at[j // ns], partner).start()
-
-        remote(give, theirs, s_rel, r_rel, sibling).start()
+                remote(send.at[j], via.at[j // ns], sent, r_via.at[j // ns], partner).start()
+
+        remote(give, theirs, sent, r_rel, sibling).start()
+        remote(shift_ref.at[0], shift_ref.at[1], sent, r_shf, sibling).start()
 
         def pass_on(i):
             wait_for(via.at[i], r_via.at[i])
@@ -607,7 +608,7 @@
 
         def result(part, core, to):
             return remote(res.at[pl.ds(per * g + quad * part, quad)], ret.at[pl.ds(quad * to, quad)],
-                          s2, r2.at[to], {"block": 2 * (across // 2) + z, "seg": x, "sub": core})
+                          sent, r2, {"block": 2 * (across // 2) + z, "seg": x, "sub": core})
 
         result(1, other, half + slot).start()
         unless_local(lambda: result(0, c, slot).start())
@@ -616,21 +617,21 @@
         def _():
             ret[0:quad] = res[per * g:per * g + quad]
 
-    for g in range(2 * half):
-        unless_here(g, lambda: wait_for(ret.at[pl.ds(quad * g, quad)], r2.at[g]))
+    pl.when(c == 0)(lambda: wait_for(ret.at[pl.ds(quad, quad * (2 * half - 1))], r2))
+    pl.when(c == 1)(lambda: wait_for(ret, r2))
     for k in range(blocks):
         out_ref[k] = ret[slots[0, k]]
-    wait_for(give, s_rel)
-    wait_for(shift_ref.at[1], s_shf)
-    wait_for(fbuf.at[pl.ds(elems, elems)], s_fld)
+    wait_for(give, sent)
+    wait_for(shift_ref.at[1], sent)
+    wait_for(fbuf.at[pl.ds(elems, elems)], sent)
 
     def finish(skip):
-        wait_for(recv.at[pl.ds(2 * rows * skip, 2 * rows * (half - skip)), :], s1)
-        wait_for(ret.at[pl.ds(quad * skip, quad * (2 * half - skip))], s2)
+        wait_for(recv.at[pl.ds(2 * rows * skip, 2 * rows * (half - skip)), :], sent)
+        wait_for(ret.at[pl.ds(quad * skip, quad * (2 * half - skip))], sent)
 
     pl.when(c == 0)(lambda: finish(1))
     pl.when(c == 1)(lambda: finish(0))
-    pl.when(first)(lambda: wait_for(via, s1))
+    pl.when(first)(lambda: wait_for(via, sent))
 
 
 def paired(sizes, old_fields, corner_shift, points, owners):
@@ -664,8 +665,7 @@
             pltpu.VMEM((3, 16 * quad, pts), F32),
             result, result,
             pltpu.SMEM((1, blocks), jnp.int32),
-            *[dma] * 4, *[dma] * 6,
-            dma, dma((half,)), dma, dma((2 * half,)),
+            *[dma] * 6, dma((half,)), dma,
             dma((half // sizes[1],)), pltpu.SemaphoreType.REGULAR((half,)),
         ],
         compiler_params=pltpu.CompilerParams(

time: 12.8 us -> 12.7 us (level)
  no operation moved by 1% of the time
where the time goes in v4:
time: 12.7 us; the launch traced here: 12.5 us
  Pallas kernels  11.9 us (94%)
  local copies, waits for them, and re-layouts  0.63 us (5%)
    pallas_call x1, Pallas kernels, paired(): pl.pallas_call(functools.partial(pair_kernel, sizes), out_shape=jax.Shape...  11.9 us
    unnamed x1, local copies, waits for them, and re-layouts  0.63 us

profile of v4, /device:TPU:0, one launch (start us, length us, event | category | flops | bytes accessed | tf_op | source)
XLA Modules:
  0.0 12.5 jit_solution(14534975672705960534)
XLA Ops:
  0.0 11.9 %shard_map.46 = f32[32,4,128]{2,1,0:T(4,128)S(1)} custom-call(s32[1,32]{1,0:T(1,128)} %bitcast.15, f32[32,3,128]{2,1,0:T(4,128)} %bitcast.14, f32[24,64]{1,0:T(8,128)} %shift_hbm.1, f32[64,16,128]{2,1,0:T(8,128)} %bitcast.13), custom_call_target="tpu_custom_call" | custom-call | tf_op jit(solution)/shard_map/pallas_call | solution.py:649
  11.9 0.6 %copy.7 = f32[4,4096]{1,0:T(4,128)} copy(f32[4,4096]{1,0:T(4,128)S(1)} %bitcast.12) | data formatting | bytes 131072

commit v5 on v4

--- a/solution.py
+++ b/solution.py
@@ -329,11 +329,11 @@
 
 def pair_kernel(sizes, owners_hbm, targets_hbm, shift_hbm, fields_hbm, out_ref,
                 owners_ref, targets_ref, shift_ref, fbuf, ctab, send, give, via, recv, cbuf, lag, res, ret, slots,
-                csem, fsem, sent, r_rel, r_shf, r_fld, r1, r2, r_via, here):
+                csem, fsem, sent, r_rel, r_fld, r1, r2, r_via, here):
     nb, ns, nc = sizes
     half = nb * ns // 2
     blocks = owners_ref.shape[1]
-    elems = shift_ref.shape[2]
+    elems = shift_ref.shape[1]
     pts = out_ref.shape[2]
     quad = nc * CAP
     rows = 4 * quad
@@ -399,7 +399,7 @@
         for j in reversed(range(1, half)):
             pl.when(above(j))(lambda: hello(near(j, 0)))
 
-    get_shift = pltpu.make_async_copy(shift_hbm, shift_ref.at[0], csem)
+    get_shift = pltpu.make_async_copy(shift_hbm, shift_ref, csem)
     get_shift.start()
     fetch = pltpu.make_async_copy(fields_hbm, fbuf.at[pl.ds(0, elems)], fsem)
     fetch.start()
@@ -407,21 +407,21 @@
     pl.when(c == 0)(lambda: pl.semaphore_wait(barrier, 1 + (b % 2) * ns + s))
     pl.when(high)(lambda: pl.semaphore_wait(barrier, half))
 
-    def answer(j, device):
-        pl.semaphore_signal(here.at[j], inc=1, device_id=device, device_id_type=pl.DeviceIdType.MESH)
+    def answer(device):
+        pl.semaphore_signal(here, inc=1, device_id=device, device_id_type=pl.DeviceIdType.MESH)
 
     @pl.when(high)
     def _():
         for j in reversed(range(half)):
             if j % ns:
-                pl.when(flip(across, j // ns) != 0)(lambda: answer(j, peer(j, 1)))
+                pl.when(flip(across, j // ns) != 0)(lambda: answer(peer(j, 1)))
             else:
-                answer(j, peer(j, 1))
+                answer(peer(j, 1))
 
     @pl.when(c == 0)
     def _():
         for j in reversed(range(1, half)):
-            pl.when(below(j))(lambda: answer(j, near(j, 0)))
+            pl.when(below(j))(lambda: answer(near(j, 0)))
 
     shift_bits = elems.bit_length() - 1
     square = (blocks, blocks)
@@ -464,14 +464,15 @@
     low_lane = iota((8, 128), 1) < 64
 
     def split(e):
-        parts = []
+        high_part, low_part = [], []
         for r in range(0, fbuf.shape[1], 8):
             x = fbuf[e, r:r + 8, :]
-            hi = x.astype(BF16).astype(F32)
-            lo = x - hi
-            turned = pltpu.roll(jnp.where(low_lane, lo, hi), 64, axis=1)
-            parts += [jnp.where(low_lane, hi, turned), jnp.where(low_lane, turned, lo)]
-        return jnp.concatenate(parts, axis=0).astype(BF16)
+            turned = pltpu.roll(x, 64, axis=1)
+            for part in (jnp.where(low_lane, x, turned), jnp.where(low_lane, turned, x)):
+                hi = part.astype(BF16).astype(F32)
+                high_part.append(hi)
+                low_part.append(part - hi)
+        return jnp.concatenate(high_part + low_part, axis=0).astype(BF16)
 
     row, col = iota((24, 24), 0), iota((24, 24), 1)
     both_bits = jnp.bitwise_and(row, col) % 8
@@ -482,18 +483,20 @@
     line = iota((24, elems), 0)
     unit = jnp.where(line % 8 == jnp.right_shift(4, line // 8), 1.0, 0.0)
 
-    def spread(side):
-        coefs = jnp.dot(hada * sign, shift_ref[side], precision=EXACT, preferred_element_type=F32) + unit
+    def spread(side, shift):
+        coefs = jnp.dot(hada * sign, shift, precision=EXACT, preferred_element_type=F32) + unit
         for e in range(elems):
             ctab[side * elems + e] = jnp.broadcast_to(coefs[:, e:e + 1], (24, pts))
 
     get_shift.wait()
+    give[half, :, :elems] = shift_ref[:rows]
+    give[half + 1, :24 - rows, :elems] = shift_ref[rows:]
     fetch.wait()
     pl.when(first)(lambda: pl.semaphore_wait(barrier, 1))
     theirs = send.at[:, pl.ds(rows, rows), :]
 
-    def heard(j):
-        pl.semaphore_wait(here.at[j], 1)
+    def heard(count):
+        pl.semaphore_wait(here, count)
 
     def share():
         remote(fbuf.at[pl.ds(0, elems)], fbuf.at[pl.ds(elems, elems)], sent, r_fld, sibling).start()
@@ -507,11 +510,10 @@
     @pl.when(c == 0)
     def _():
         remote(give, theirs, sent, r_rel, sibling).start()
-        remote(shift_ref.at[0], shift_ref.at[1], sent, r_shf, sibling).start()
         share()
         wait_for(theirs, r_rel)
+        pl.when(corner < half - 1)(lambda: heard(half - 1 - corner))
         for j in reversed(range(1, half)):
-            pl.when(above(j))(lambda: heard(j))
             request(send.at[j], corner, near(j, 0))
         recv[pl.ds(pl.multiple_of(2 * rows * corner, 2 * rows), 2 * rows), :] = send[0]
 
@@ -522,13 +524,11 @@
         @pl.when(b == 0)
         def _():
             for j in reversed(range(1, half, ns)):
-                remote(send.at[j], via.at[j // ns], sent, r_via.at[j // ns], partner).start()
+                remote(send.at[j], via.at[j // ns], sent, r_via, partner).start()
 
         remote(give, theirs, sent, r_rel, sibling).start()
-        remote(shift_ref.at[0], shift_ref.at[1], sent, r_shf, sibling).start()
 
         def pass_on(i):
-            wait_for(via.at[i], r_via.at[i])
             request(via.at[i], flip(s, 1), peer(ns * i, 1))
 
         def own(i):
@@ -538,31 +538,32 @@
 
         @pl.when(jnp.logical_and(b == 0, s == 0))
         def _():
+            heard(half // ns)
             for i in columns:
-                heard(ns * i)
                 own(i)
             share()
+            wait_for(via, r_via)
             for i in columns:
                 pass_on(i)
 
         @pl.when(jnp.logical_and(b == 0, s == 1))
         def _():
+            wait_for(via, r_via)
+            heard(half // ns)
             for i in columns:
-                heard(ns * i)
                 pass_on(i)
                 own(i)
             share()
 
         @pl.when(b > 0)
         def _():
+            pl.when(b < top)(lambda: heard(half))
             for j in reversed(range(half)):
-                pl.when(b < top)(lambda: heard(j))
                 request(send.at[j], corner, peer(j, 1))
             share()
 
-    spread(0)
-    wait_for(shift_ref.at[1], r_shf)
-    spread(1)
+    spread(0, shift_ref[...])
+    spread(1, jnp.concatenate([send[half, rows:2 * rows, :elems], send[half + 1, rows:2 * rows, :elems]], axis=0)[:24])
     wait_for(fbuf.at[pl.ds(elems, elems)], r_fld)
 
     for g in range(half):
@@ -592,10 +593,8 @@
             w = jnp.concatenate([lag[1, 8 * k + i:8 * k + i + 1, :] * lz for i in range(8)], axis=0)
             w_hi = w.astype(BF16)
             w_lo = (w - w_hi.astype(F32)).astype(BF16)
-            prod = jnp.dot(
-                jnp.concatenate([left, left], axis=1),
-                jnp.concatenate([w_hi, w_hi, w_lo, w_lo], axis=0),
-                preferred_element_type=F32)
+            prod = jnp.dot(left, jnp.concatenate([w_hi, w_lo], axis=0), preferred_element_type=F32)
+            prod = prod[:32] + prod[32:]
             total = None
             for q in range(4):
                 i = 8 * k + 4 * (q // 2) + q % 2
@@ -622,7 +621,6 @@
     for k in range(blocks):
         out_ref[k] = ret[slots[0, k]]
     wait_for(give, sent)
-    wait_for(shift_ref.at[1], sent)
     wait_for(fbuf.at[pl.ds(elems, elems)], sent)
 
     def finish(skip):
@@ -654,19 +652,19 @@
         scratch_shapes=[
             pltpu.VMEM((1, blocks), jnp.int32),
             pltpu.VMEM((blocks, 3, pts), F32),
-            pltpu.VMEM((2, 24, elems), F32),
+            pltpu.VMEM((24, elems), F32),
             pltpu.VMEM((2 * elems, nvar * nodes // 128, 128), F32),
             pltpu.VMEM((2 * elems, 24, pts), F32),
-            pltpu.VMEM((half, 2 * rows, pts), F32),
-            pltpu.VMEM((half, rows, pts), F32),
+            pltpu.VMEM((half + 2, 2 * rows, pts), F32),
+            pltpu.VMEM((half + 2, rows, pts), F32),
             pltpu.VMEM((half // sizes[1], 2 * rows, pts), F32),
             pltpu.VMEM((2 * rows * half, pts), F32),
             pltpu.VMEM((3, 16 * quad, pts), F32),
             pltpu.VMEM((3, 16 * quad, pts), F32),
             result, result,
             pltpu.SMEM((1, blocks), jnp.int32),
-            *[dma] * 6, dma((half,)), dma,
-            dma((half // sizes[1],)), pltpu.SemaphoreType.REGULAR((half,)),
+            *[dma] * 5, dma((half,)), dma,
+            dma, pltpu.SemaphoreType.REGULAR,
         ],
         compiler_params=pltpu.CompilerParams(
             collective_id=0, has_side_effects=True, vmem_limit_bytes=24 * 1024 * 1024),

time: 12.7 us -> 12.7 us (level)
  no operation moved by 1% of the time
where the time goes in v5:
time: 12.7 us; the launch traced here: 12.5 us
  Pallas kernels  11.9 us (94%)
  local copies, waits for them, and re-layouts  0.63 us (5%)
    pallas_call x1, Pallas kernels, paired(): pl.pallas_call(functools.partial(pair_kernel, sizes), out_shape=jax.Shape...  11.9 us
    unnamed x1, local copies, waits for them, and re-layouts  0.63 us

profile of v5, /device:TPU:0, one launch (start us, length us, event | category | flops | bytes accessed | tf_op | source)
XLA Modules:
  0.0 12.5 jit_solution(11169355177494825036)
XLA Ops:
  0.0 11.9 %shard_map.46 = f32[32,4,128]{2,1,0:T(4,128)S(1)} custom-call(s32[1,32]{1,0:T(1,128)} %bitcast.15, f32[32,3,128]{2,1,0:T(4,128)} %bitcast.14, f32[24,64]{1,0:T(8,128)} %shift_hbm.1, f32[64,16,128]{2,1,0:T(8,128)} %bitcast.13), custom_call_target="tpu_custom_call" | custom-call | tf_op jit(solution)/shard_map/pallas_call | solution.py:647
  11.9 0.6 %copy.7 = f32[4,4096]{1,0:T(4,128)} copy(f32[4,4096]{1,0:T(4,128)S(1)} %bitcast.12) | data formatting | bytes 131072

commit v6 on v5

--- a/solution.py
+++ b/solution.py
@@ -507,6 +507,15 @@
         at = pl.multiple_of(2 * rows * group, 2 * rows)
         remote(src, recv.at[pl.ds(at, 2 * rows), :], sent, r1.at[group], device).start()
 
+    def parted(src, device, core):
+        for part, sem in ((core, 0), (1 - core, half)):
+            piece = pl.ds(rows * part, rows)
+            remote(src.at[piece, :], recv.at[piece, :], sent, r1.at[sem], device).start()
+
+    def mine(src, device, core):
+        pl.when(corner == 0)(lambda: parted(src, device, core))
+        pl.when(corner > 0)(lambda: request(src, corner, device))
+
     @pl.when(c == 0)
     def _():
         remote(give, theirs, sent, r_rel, sibling).start()
@@ -514,7 +523,7 @@
         wait_for(theirs, r_rel)
         pl.when(corner < half - 1)(lambda: heard(half - 1 - corner))
         for j in reversed(range(1, half)):
-            request(send.at[j], corner, near(j, 0))
+            mine(send.at[j], near(j, 0), 0)
         recv[pl.ds(pl.multiple_of(2 * rows * corner, 2 * rows), 2 * rows), :] = send[0]
 
     @pl.when(c == 1)
@@ -528,93 +537,101 @@
 
         remote(give, theirs, sent, r_rel, sibling).start()
 
-        def pass_on(i):
-            request(via.at[i], flip(s, 1), peer(ns * i, 1))
-
-        def own(i):
-            request(send.at[ns * i], corner, peer(ns * i, 1))
-
         columns = list(reversed(range(half // ns)))
 
         @pl.when(jnp.logical_and(b == 0, s == 0))
         def _():
             heard(half // ns)
             for i in columns:
-                own(i)
+                parted(send.at[ns * i], peer(ns * i, 1), 1)
             share()
             wait_for(via, r_via)
             for i in columns:
-                pass_on(i)
+                request(via.at[i], 1, peer(ns * i, 1))
 
         @pl.when(jnp.logical_and(b == 0, s == 1))
         def _():
             wait_for(via, r_via)
             heard(half // ns)
             for i in columns:
-                pass_on(i)
-                own(i)
+                parted(via.at[i], peer(ns * i, 1), 1)
+                request(send.at[ns * i], 1, peer(ns * i, 1))
             share()
 
         @pl.when(b > 0)
         def _():
             pl.when(b < top)(lambda: heard(half))
             for j in reversed(range(half)):
-                request(send.at[j], corner, peer(j, 1))
+                mine(send.at[j], peer(j, 1), 1)
             share()
 
     spread(0, shift_ref[...])
     spread(1, jnp.concatenate([send[half, rows:2 * rows, :elems], send[half + 1, rows:2 * rows, :elems]], axis=0)[:24])
     wait_for(fbuf.at[pl.ds(elems, elems)], r_fld)
 
-    for g in range(half):
-        base = 2 * rows * g
-        z, x = g // ns, g % ns
-        local = jnp.logical_and(c == 0, corner == g)
-
-        def unless_local(body):
-            pl.when(jnp.logical_not(local))(body)
-
-        unless_local(lambda: wait_for(recv.at[pl.ds(base, 2 * rows), :], r1.at[g]))
-        y = [recv[pl.ds(base + a, per, stride=4), :] for a in range(3)]
-        ids = recv[pl.ds(base + 3, per, stride=4), :].astype(jnp.int32)
+    def compute(base, count, at):
+        y = [recv[pl.ds(base + a, count, stride=4), :] for a in range(3)]
+        ids = recv[pl.ds(base + 3, count, stride=4), :].astype(jnp.int32)
         ids = jnp.minimum(jnp.maximum(ids, 0), 2 * elems - 1)
-        elem = [ids[k, 0] for k in range(per)]
-        for k in range(per):
+        elem = [ids[k, 0] for k in range(count)]
+        for k in range(count):
             for a in range(3):
                 cbuf[a, 8 * k:8 * k + 8, :] = ctab[elem[k], 8 * a:8 * a + 8, :]
-        coef = [[cbuf[a, pl.ds(m, per, stride=8), :] for m in range(8)] for a in range(3)]
+        coef = [[cbuf[a, pl.ds(m, count, stride=8), :] for m in range(8)] for a in range(3)]
         xi = newton(coef, y)
         for a in range(3):
             for i, value in enumerate(lagrange(xi[a])):
-                lag[a, pl.ds(i, per, stride=8), :] = value
-        for k in range(per):
+                lag[a, per * i:per * i + count, :] = value
+        for k in range(count):
             left = split(elem[k])
-            lz = lag[2, 8 * k:8 * k + 8, :]
-            w = jnp.concatenate([lag[1, 8 * k + i:8 * k + i + 1, :] * lz for i in range(8)], axis=0)
+            lz = lag[2, pl.ds(k, 8, stride=per), :]
+            w = jnp.concatenate([lag[1, per * i + k:per * i + k + 1, :] * lz for i in range(8)], axis=0)
             w_hi = w.astype(BF16)
             w_lo = (w - w_hi.astype(F32)).astype(BF16)
             prod = jnp.dot(left, jnp.concatenate([w_hi, w_lo], axis=0), preferred_element_type=F32)
             prod = prod[:32] + prod[32:]
             total = None
             for q in range(4):
-                i = 8 * k + 4 * (q // 2) + q % 2
-                lx = jnp.where(low_sub, lag[0, i:i + 1, :], lag[0, i + 2:i + 3, :])
+                i = per * (4 * (q // 2) + q % 2) + k
+                lx = jnp.where(low_sub, lag[0, i:i + 1, :], lag[0, i + 2 * per:i + 2 * per + 1, :])
                 term = prod[8 * q:8 * q + 8] * lx
                 total = term if total is None else total + term
-            res[per * g + k] = total[0:4] + total[4:8]
+            res[at + k] = total[0:4] + total[4:8]
+
+    for g in range(half):
+        base = 2 * rows * g
+        z, x = g // ns, g % ns
+        local = jnp.logical_and(c == 0, corner == g)
+
+        def unless_local(body):
+            pl.when(jnp.logical_not(local))(body)
 
         slot = ns * flip(b % 2, z) + flip(s, x)
 
-        def result(part, core, to):
-            return remote(res.at[pl.ds(per * g + quad * part, quad)], ret.at[pl.ds(quad * to, quad)],
+        def result(at, to, core):
+            return remote(res.at[pl.ds(at, quad)], ret.at[pl.ds(quad * to, quad)],
                           sent, r2, {"block": 2 * (across // 2) + z, "seg": x, "sub": core})
 
-        result(1, other, half + slot).start()
-        unless_local(lambda: result(0, c, slot).start())
-
-        @pl.when(local)
-        def _():
-            ret[0:quad] = res[per * g:per * g + quad]
+        def keep(at):
+            ret[0:quad] = res[at:at + quad]
+
+        if g == 0:
+            for part, sem in ((c, 0), (other, half)):
+                start = pl.multiple_of(rows * part, rows)
+                unless_local(lambda: wait_for(recv.at[pl.ds(start, rows), :], r1.at[sem]))
+                at = quad if sem else 0
+                compute(start, quad, at)
+                if sem:
+                    result(at, half * other + slot, 1).start()
+                else:
+                    unless_local(lambda: result(at, half * c + slot, 0).start())
+                    pl.when(local)(lambda: keep(at))
+        else:
+            unless_local(lambda: wait_for(recv.at[pl.ds(base, 2 * rows), :], r1.at[g]))
+            compute(base, per, per * g)
+            result(per * g + quad, half + slot, other).start()
+            unless_local(lambda: result(per * g, slot, c).start())
+            pl.when(local)(lambda: keep(per * g))
 
     pl.when(c == 0)(lambda: wait_for(ret.at[pl.ds(quad, quad * (2 * half - 1))], r2))
     pl.when(c == 1)(lambda: wait_for(ret, r2))
@@ -663,7 +680,7 @@
             pltpu.VMEM((3, 16 * quad, pts), F32),
             result, result,
             pltpu.SMEM((1, blocks), jnp.int32),
-            *[dma] * 5, dma((half,)), dma,
+            *[dma] * 5, dma((half + 1,)), dma,
             dma, pltpu.SemaphoreType.REGULAR,
         ],
         compiler_params=pltpu.CompilerParams(

time: 12.7 us -> 12.5 us (0.984)
  Pallas kernels: 11.9 us -> 11.7 us
    pallas_call x1, Pallas kernels: 11.9 us -> 11.7 us  [paired(): pl.pallas_call(functools.partial(pair_kernel, sizes), out_shape=jax.Shape...]
where the time goes in v6:
time: 12.5 us; the launch traced here: 12.3 us
  Pallas kernels  11.7 us (94%)
  local copies, waits for them, and re-layouts  0.63 us (5%)
    pallas_call x1, Pallas kernels, paired(): pl.pallas_call(functools.partial(pair_kernel, sizes), out_shape=jax.Shape...  11.7 us
    unnamed x1, local copies, waits for them, and re-layouts  0.63 us

profile of v6, /device:TPU:0, one launch (start us, length us, event | category | flops | bytes accessed | tf_op | source)
XLA Modules:
  0.0 12.3 jit_solution(1653983574280085561)
XLA Ops:
  0.0 11.7 %shard_map.46 = f32[32,4,128]{2,1,0:T(4,128)S(1)} custom-call(s32[1,32]{1,0:T(1,128)} %bitcast.15, f32[32,3,128]{2,1,0:T(4,128)} %bitcast.14, f32[24,64]{1,0:T(8,128)} %shift_hbm.1, f32[64,16,128]{2,1,0:T(8,128)} %bitcast.13), custom_call_target="tpu_custom_call" | custom-call | tf_op jit(solution)/shard_map/pallas_call | solution.py:664
  11.7 0.6 %copy.7 = f32[4,4096]{1,0:T(4,128)} copy(f32[4,4096]{1,0:T(4,128)S(1)} %bitcast.12) | data formatting | bytes 131072

commit v7 on v6

--- a/solution.py
+++ b/solution.py
@@ -389,7 +389,15 @@
         @pl.when(b < top)
         def _():
             for j in reversed(range(half)):
-                hello(peer(j, 1))
+                if j % ns:
+                    pl.when(s == 0)(lambda: hello(peer(j, 1)))
+                else:
+                    hello(peer(j, 1))
+
+        @pl.when(jnp.logical_and(b >= top, s == 0))
+        def _():
+            for j in reversed(range(1, half, ns)):
+                pl.when(flip(across, j // ns) != 0)(lambda: hello(peer(j, 1)))
 
         pl.when(b == 0)(lambda: hello(partner))
         hello(sibling)
@@ -405,7 +413,7 @@
     fetch.start()
 
     pl.when(c == 0)(lambda: pl.semaphore_wait(barrier, 1 + (b % 2) * ns + s))
-    pl.when(high)(lambda: pl.semaphore_wait(barrier, half))
+    pl.when(high)(lambda: pl.semaphore_wait(barrier, half // ns * (1 + s)))
 
     def answer(device):
         pl.semaphore_signal(here, inc=1, device_id=device, device_id_type=pl.DeviceIdType.MESH)
@@ -414,7 +422,7 @@
     def _():
         for j in reversed(range(half)):
             if j % ns:
-                pl.when(flip(across, j // ns) != 0)(lambda: answer(peer(j, 1)))
+                pl.when(jnp.logical_and(flip(across, j // ns) != 0, s == 1))(lambda: answer(peer(j, 1)))
             else:
                 answer(peer(j, 1))
 
@@ -493,6 +501,13 @@
     give[half + 1, :24 - rows, :elems] = shift_ref[rows:]
     fetch.wait()
     pl.when(first)(lambda: pl.semaphore_wait(barrier, 1))
+
+    @pl.when(jnp.logical_and(c == 1, jnp.logical_and(jnp.logical_and(b > 0, b < top), s == 1)))
+    def _():
+        pl.semaphore_wait(barrier, half // ns)
+        for j in reversed(range(1, half, ns)):
+            answer(peer(j, 1))
+
     theirs = send.at[:, pl.ds(rows, rows), :]
 
     def heard(count):
@@ -544,6 +559,8 @@
             heard(half // ns)
             for i in columns:
                 parted(send.at[ns * i], peer(ns * i, 1), 1)
+            for i in columns:
+                answer(peer(ns * i, 1))
             share()
             wait_for(via, r_via)
             for i in columns:
@@ -560,7 +577,8 @@
 
         @pl.when(b > 0)
         def _():
-            pl.when(b < top)(lambda: heard(half))
+            pl.when(b < top)(lambda: heard(half // ns * (2 - s)))
+            pl.when(jnp.logical_and(b >= top, s == 0))(lambda: heard(ns))
             for j in reversed(range(half)):
                 mine(send.at[j], peer(j, 1), 1)
             share()

time: 12.5 us -> 12.4 us (level)
  no operation moved by 1% of the time
where the time goes in v7:
time: 12.4 us; the launch traced here: 12.2 us
  Pallas kernels  11.6 us (94%)
  local copies, waits for them, and re-layouts  0.63 us (5%)
    pallas_call x1, Pallas kernels, paired(): pl.pallas_call(functools.partial(pair_kernel, sizes), out_shape=jax.Shape...  11.6 us
    unnamed x1, local copies, waits for them, and re-layouts  0.63 us

profile of v7, /device:TPU:0, one launch (start us, length us, event | category | flops | bytes accessed | tf_op | source)
XLA Modules:
  0.0 12.2 jit_solution(15428145597890244058)
XLA Ops:
  0.0 11.6 %shard_map.46 = f32[32,4,128]{2,1,0:T(4,128)S(1)} custom-call(s32[1,32]{1,0:T(1,128)} %bitcast.15, f32[32,3,128]{2,1,0:T(4,128)} %bitcast.14, f32[24,64]{1,0:T(8,128)} %shift_hbm.1, f32[64,16,128]{2,1,0:T(8,128)} %bitcast.13), custom_call_target="tpu_custom_call" | custom-call | tf_op jit(solution)/shard_map/pallas_call | solution.py:682
  11.6 0.6 %copy.7 = f32[4,4096]{1,0:T(4,128)} copy(f32[4,4096]{1,0:T(4,128)S(1)} %bitcast.12) | data formatting | bytes 131072

commit v8 on v7

--- a/solution.py
+++ b/solution.py
@@ -572,6 +572,7 @@
             heard(half // ns)
             for i in columns:
                 parted(via.at[i], peer(ns * i, 1), 1)
+            for i in columns:
                 request(send.at[ns * i], 1, peer(ns * i, 1))
             share()
 

time: 12.4 us -> 12.5 us (level)
  no operation moved by 1% of the time
where the time goes in v8:
time: 12.5 us; the launch traced here: 12.3 us
  Pallas kernels  11.7 us (94%)
  local copies, waits for them, and re-layouts  0.63 us (5%)
    pallas_call x1, Pallas kernels, paired(): pl.pallas_call(functools.partial(pair_kernel, sizes), out_shape=jax.Shape...  11.7 us
    unnamed x1, local copies, waits for them, and re-layouts  0.63 us

profile of v8, /device:TPU:0, one launch (start us, length us, event | category | flops | bytes accessed | tf_op | source)
XLA Modules:
  0.0 12.3 jit_solution(11951016803753194962)
XLA Ops:
  0.0 11.7 %shard_map.46 = f32[32,4,128]{2,1,0:T(4,128)S(1)} custom-call(s32[1,32]{1,0:T(1,128)} %bitcast.15, f32[32,3,128]{2,1,0:T(4,128)} %bitcast.14, f32[24,64]{1,0:T(8,128)} %shift_hbm.1, f32[64,16,128]{2,1,0:T(8,128)} %bitcast.13), custom_call_target="tpu_custom_call" | custom-call | tf_op jit(solution)/shard_map/pallas_call | solution.py:683
  11.7 0.6 %copy.7 = f32[4,4096]{1,0:T(4,128)} copy(f32[4,4096]{1,0:T(4,128)S(1)} %bitcast.12) | data formatting | bytes 131072
